TPU v7x, 256 devices: a whole 4x4x8 slice. The times are simulated.
256 devices in a mesh: dp: 16 (over z, core), expert: 16 (over y, x).
Axes of the slice: x: 4, y: 4, z: 8, core: 2. Of those that a mesh axis runs over, the one named last changes fastest.
Arguments:
- tokens: bfloat16 [131072, 2048], P(('dp', 'expert')), parts along dimension 0, may hold values from -6 to 6
- modality: int32 [131072], P(('dp', 'expert')), parts along dimension 0, may hold values 0 or 1
- expert_ids: int32 [131072, 2], P(('dp', 'expert')), parts along dimension 0, may hold values from 0 to 15, all different within a row; in each aligned block of 512 rows (0 to 511, 512 to 1023, ...) at most 80 rows name the same one
- route_weights: float32 [131072, 2], P(('dp', 'expert')), parts along dimension 0, may hold values from 0.25 to 1
- norm_gain: float32 [2, 2048], replicated, may hold values from 0.25 to 1.75
- gate_weight: bfloat16 [2048, 14336], P(None, 'expert'), may hold values from -0.125 to 0.125
- up_weight: bfloat16 [2048, 14336], P(None, 'expert'), may hold values from -0.125 to 0.125
- down_weight: bfloat16 [14336, 2048], P('expert'), may hold values from -0.1875 to 0.1875
Outputs:
- mixed: bfloat16 [131072, 2048], P(('dp', 'expert')), parts along dimension 0
There are 16 independent parts, one for each index of `dp`. A program takes and returns all parts, laid end to end along the dimension named above; an argument that names none is the same for every part. Nothing has to cross between parts.
Inputs may be any that keep to these rules, and one draw needn't show every extreme that they name: `expert_ids`: each row names 2 different experts. Among the rows of one device no expert is named by more than 80 rows, a bound that some blocks reach.
All inputs are finite; a program needn't handle non-finite values. No bound on the sum of `modality` on one device may be relied on, other than what follows from the above.
Results may differ from a plain program's by a relative error of at most 0.0054.
Values may be sent and summed in bfloat16 or wider, within the bound.
A program may use at most 128 MiB of HBM per device.

v0:
```python
import jax
import jax.numpy as jnp
from jax import lax
from jax.sharding import PartitionSpec as P

epsilon = 1e-05


def normalize(tokens, modality, norm_gain):
    values = tokens.astype(jnp.float32)
    square = jnp.mean(values * values, axis=1, keepdims=True)
    gains = jnp.where(modality[:, None] == 1, norm_gain[1][None, :], norm_gain[0][None, :])
    return (values * lax.rsqrt(square + epsilon) * gains).astype(jnp.bfloat16)


def slot_table(expert_ids, experts, capacity):
    fanout = expert_ids.shape[1]
    flat_ids = expert_ids.reshape(-1)
    columns = jnp.arange(experts, dtype=jnp.int32)
    onehot = (flat_ids[:, None] == columns[None, :]).astype(jnp.int32)
    earlier = jnp.cumsum(onehot, axis=0) - onehot
    position = jnp.sum(earlier * onehot, axis=1)
    slots = flat_ids * capacity + position
    sources = jnp.arange(flat_ids.shape[0], dtype=jnp.int32) // fanout
    owners = jnp.full((experts * capacity,), -1, jnp.int32).at[slots].set(sources)
    return (slots, owners)


def pack_rows(normed, owners):
    chosen = jnp.take(normed, jnp.maximum(owners, 0), axis=0)
    return jnp.where(owners[:, None] >= 0, chosen, jnp.zeros_like(chosen))


def expert_rows(rows, gate_weight, up_weight, down_weight):
    leading = rows.shape[:-1]
    flat = rows.reshape(-1, rows.shape[-1])
    gate = jnp.dot(flat, gate_weight, preferred_element_type=jnp.float32)
    upper = jnp.dot(flat, up_weight, preferred_element_type=jnp.float32)
    active = (jax.nn.silu(gate) * upper).astype(jnp.bfloat16)
    result = jnp.dot(active, down_weight, preferred_element_type=jnp.float32).astype(jnp.bfloat16)
    return result.reshape(leading + (down_weight.shape[1],))


def shards(
    tokens, modality, expert_ids, route_weights, norm_gain, gate_weight, up_weight, down_weight
):
    devices = lax.axis_size("expert")
    tok_rows, width = tokens.shape
    fanout = expert_ids.shape[1]
    capacity = min(tok_rows, tok_rows * fanout * 5 // (4 * devices))
    normed = normalize(tokens, modality, norm_gain)
    slots, owners = slot_table(expert_ids, devices, capacity)
    blocks = pack_rows(normed, owners).reshape(devices, capacity, width)
    finished = expert_rows(
        lax.all_to_all(blocks, "expert", split_axis=0, concat_axis=0, tiled=True),
        gate_weight,
        up_weight,
        down_weight,
    )
    returned = lax.all_to_all(finished, "expert", split_axis=0, concat_axis=0, tiled=True)
    expert_out = returned.reshape(devices * capacity, width)
    picked = (
        jnp.take(expert_out, slots, axis=0).reshape(tok_rows, fanout, width).astype(jnp.float32)
    )
    mixed = tokens.astype(jnp.float32) + jnp.sum(route_weights[:, :, None] * picked, axis=1)
    return mixed.astype(jnp.bfloat16)


def solution(mesh):
    placed = (
        P(("dp", "expert"), None),
        P(("dp", "expert")),
        P(("dp", "expert"), None),
        P(("dp", "expert"), None),
        P(),
        P(None, "expert"),
        P(None, "expert"),
        P("expert", None),
    )
    return jax.shard_map(
        shards, mesh=mesh, in_specs=placed, out_specs=P(("dp", "expert"), None), check_vma=False
    )
```

profile of v0, /device:TPU:1, one launch (start us, length us, event | category | flops | bytes accessed | tf_op | source)
XLA Modules:
  0.0 242.3 jit_solution(3083578734960924755)
XLA Ops:
  0.0 0.8 copy.20
  0.8 0.2 eq.33
  1.0 0.2 reshape.101
  1.2 0.7 broadcast_multiply_fusion
  1.9 4.5 %reduce-window.6 = s32[16,8,128]{2,1,0:T(8,128)S(1)} reduce-window(s32[16,8,128]{2,1,0:T(8,128)S(1)} %fusion.7, s32[]{:T(128)} %constant.59.clone.1), window={size=1x1x128 pad=0_0x0_0x127_0}, to_apply=%region_0.0 | reduce-window | flops 2080768 | bytes 131076 | tf_op jit(solution)/shard_map/reduce-window
  7.0 0.2 mul.55
  7.2 4.3 %scatter_custom_fusion = s32[1280]{0:T(1024)S(1)} fusion(s32[1024]{0:T(1024)S(1)} %bitcast.40, s32[1024]{0:T(1024)S(1)} %add_select_fusion, s32[]{:T(128)} %constant.62.clone.1), kind=kCustom, calls=%fused_computation.36 | custom fusion | bytes 5124 | tf_op jit(solution)/shard_map/scatter | solution.py:25
  11.6 0.8 fusion.14
  12.4 2.1 fusion
  14.7 2.4 fusion.2
  17.1 6.1 %gather_fusion = bf16[1280,2048]{1,0:T(8,128)(2,1)} fusion(bf16[512,2048]{1,0:T(8,128)(2,1)S(1)} %fusion.2, s32[2048]{0:T(1024)S(1)} %pad_clamp_fusion), kind=kCustom, calls=%fused_computation | custom fusion | bytes 10490880 | tf_op jit(solution)/shard_map/jit(_take)/gather | solution.py:30
  23.2 2.9 %select_select_fusion = bf16[16,80,2048]{2,1,0:T(8,128)(2,1)S(1)} fusion(bf16[16,80,2048]{2,1,0:T(8,128)(2,1)} %bitcast.31, pred[16,80]{1,0:T(8,128)(4,1)S(1)} %broadcast_in_dim.78, pred[16,80]{1,0:T(8,128)(4,1)S(1)} %broadcast_in_dim.76), kind=kLoop, calls=%fused_computation.9 | loop fusion | flops 5242880 | bytes 10488320 | tf_op jit(solution)/shard_map/jit(_where)/select_n | solution.py:31
  26.2 68.6 %all_to_all.10 = bf16[16,80,2048]{2,1,0:T(8,128)(2,1)S(1)} all-to-all(bf16[16,80,2048]{2,1,0:T(8,128)(2,1)S(1)} %select_select_fusion), channel_id=1, replica_groups=mesh['dp'=16,'expert'=16] {'expert'}, dimensions={0} | all-to-all | bytes 10485760 | tf_op jit(solution)/shard_map/all_to_all | solution.py:55
  94.8 2.3 copy-done.1
  97.1 7.1 %fusion.15 = f32[1280,896]{1,0:T(8,128)} fusion(bf16[1280,2048]{1,0:T(8,128)(2,1)S(1)} %bitcast.33, bf16[2048,896]{1,0:T(8,128)(2,1)S(1)} %copy-done.5), kind=kOutput, calls=%fused_computation.45 | convolution fusion | flops 4697620480 | bytes 13500416 | tf_op jit(solution)/shard_map/dot_general | solution.py:37
  104.3 17.5 %convolution_convert_fusion = bf16[1280,2048]{1,0:T(8,128)(2,1)} fusion(bf16[896,2048]{1,0:T(8,128)(2,1)} %param.15, f32[1280,896]{1,0:T(8,128)} %fusion.15, bf16[1280,2048]{1,0:T(8,128)(2,1)} %bitcast.34, bf16[2048,896]{1,0:T(8,128)(2,1)} %param.14), kind=kOutput, calls=%fused_computation.5 | convolution fusion | flops 9404743680 | bytes 22413312 | tf_op jit(solution)/shard_map/dot_general | solution.py:40
  121.8 4.9 %all-to-all-start.1 = ((bf16[16,80,2048]{2,1,0:T(8,128)(2,1)}), bf16[16,80,2048]{2,1,0:T(8,128)(2,1)}, u32[]{:S(2)}, u32[]{:S(2)}) async-start(bf16[16,80,2048]{2,1,0:T(8,128)(2,1)} %bitcast.32), calls=%async_computation.1 | async-start | bytes 10485760 | tf_op jit(solution)/shard_map/all_to_all | solution.py:60
  126.7 0.2 reduce_sum.32
  127.1 0.2 copy.25
  127.4 74.1 %all-to-all-done.1 = bf16[16,80,2048]{2,1,0:T(8,128)(2,1)} async-done(((bf16[16,80,2048]{2,1,0:T(8,128)(2,1)}), bf16[16,80,2048]{2,1,0:T(8,128)(2,1)}, u32[]{:S(2)}, u32[]{:S(2)}) %all-to-all-start.1) | async-done | bytes 5242912 | tf_op jit(solution)/shard_map/all_to_all | solution.py:60
  201.6 12.0 %gather_fusion.1 = bf16[1024,2048]{1,0:T(8,128)(2,1)} fusion(bf16[1280,2048]{1,0:T(8,128)(2,1)} %bitcast.9, s32[1024]{0:T(1024)S(1)} %broadcast_clamp_fusion), kind=kCustom, calls=%fused_computation.1 | custom fusion | bytes 8392704 | tf_op jit(solution)/shard_map/jit(_take)/gather | solution.py:63
  213.5 7.6 %gather.15 = bf16[512,2,2048]{2,1,0:T(2,128)(2,1)} reshape(bf16[1024,2048]{1,0:T(8,128)(2,1)} %gather_fusion.1) | data formatting | bytes 8388608 | tf_op jit(solution)/shard_map/jit(_take)/gather | solution.py:63
  221.2 19.0 %multiply_reduce_fusion = f32[512,2048]{1,0:T(8,128)S(1)} fusion(bf16[512,2,2048]{2,1,0:T(2,128)(2,1)} %gather.15, pred[512,2]{1,0:T(8,128)(4,1)S(1)} %copy.25, f32[512,2]{1,0:T(8,128)S(1)} %copy.19), kind=kLoop, calls=%fused_computation.3 | loop fusion | flops 7340032 | bytes 8393728 | tf_op jit(solution)/shard_map/reduce_sum | solution.py:65
  240.2 2.1 fusion.3
  (33 shorter events, 1.1 us)
Async XLA Ops:
  0.0 14.5 %copy-start.4 = (s32[512]{0:T(512)S(1)}, s32[512]{0:T(512)}, u32[]{:S(2)}) copy-start(s32[512]{0:T(512)} %param.9) | copy-start | bytes 6148
  26.2 71.0 %copy-start.5 = (bf16[2048,896]{1,0:T(8,128)(2,1)S(1)}, bf16[2048,896]{1,0:T(8,128)(2,1)}, u32[]{:S(2)}) copy-start(bf16[2048,896]{1,0:T(8,128)(2,1)} %param.13) | copy-start | bytes 11010052
  94.8 2.3 copy-start.1
  121.8 5.2 %copy-start.2 = (s32[512,2]{0,1:T(2,128)S(1)}, s32[512,2]{0,1:T(2,128)}, u32[]{:S(2)}) copy-start(s32[512,2]{0,1:T(2,128)} %param.10) | copy-start | bytes 12292
  121.8 5.5 %copy-start.3 = (f32[512,2]{0,1:T(2,128)S(1)}, f32[512,2]{0,1:T(2,128)}, u32[]{:S(2)}) copy-start(f32[512,2]{0,1:T(2,128)} %param.11) | copy-start | bytes 12292
  121.8 79.7 %all-to-all-start.1 = ((bf16[16,80,2048]{2,1,0:T(8,128)(2,1)}), bf16[16,80,2048]{2,1,0:T(8,128)(2,1)}, u32[]{:S(2)}, u32[]{:S(2)}) async-start(bf16[16,80,2048]{2,1,0:T(8,128)(2,1)} %bitcast.32), calls=%async_computation.1 | async-start | bytes 10485760 | tf_op jit(solution)/shard_map/all_to_all | solution.py:60
  221.2 19.0 %copy-start = (bf16[512,2048]{1,0:T(8,128)(2,1)S(1)}, bf16[512,2048]{1,0:T(8,128)(2,1)}, u32[]{:S(2)}) copy-start(bf16[512,2048]{1,0:T(8,128)(2,1)} %param.8) | copy-start | bytes 6291460
where the time goes:
time: 244 us; the launch traced here: 242 us
  waiting for transfers between devices  74.1 us (30%)
  blocking collectives  68.6 us (28%)
  local copies, waits for them, and re-layouts  35.8 us (15%)
  other arithmetic  33.9 us (14%)
  matrix products  24.7 us (10%)
  starting transfers between devices  4.91 us (2%)
    all_to_all x1, waiting for transfers between devices, shards(): lax.all_to_all(finished, 'expert', split_axis=0, concat_axis=0, tiled=True)  74.1 us
    all_to_all x1, blocking collectives, shards(): lax.all_to_all(blocks, 'expert', split_axis=0, concat_axis=0, tiled=True)  68.6 us
    gather x2, local copies, waits for them, and re-layouts, shards(): jnp.take(expert_out, slots, axis=0).reshape(tok_rows, fanout, width)  19.6 us
    reduce_sum x1, other arithmetic, shards(): jnp.sum(route_weights[:, :, None] * picked, axis=1)  19 us
    dot_general x1, matrix products, expert_rows(): jnp.dot(active, down_weight, preferred_element_type=jnp.float32)  17.5 us
    dot_general x1, matrix products, expert_rows(): gate = jnp.dot(flat, gate_weight, preferred_element_type=jnp.float32)  7.14 us
    gather x1, local copies, waits for them, and re-layouts, pack_rows(): chosen = jnp.take(normed, jnp.maximum(owners, 0), axis=0)  6.12 us
    all_to_all x1, starting transfers between devices, shards(): lax.all_to_all(finished, 'expert', split_axis=0, concat_axis=0, tiled=True)  4.91 us
  transfers between devices with their start and end apart: 1, of which 1 were waited for; matrix products, arithmetic and copies ran while one was open for 0% of the time, Pallas kernels for 0%

commit v1 on v0

v1 whole, which is shorter than its diff:
```python
import functools

import jax
import jax.numpy as jnp
from jax import lax
from jax.experimental import pallas as pl
from jax.experimental.pallas import tpu as pltpu
from jax.sharding import PartitionSpec as P

MESH = pl.DeviceIdType.MESH
epsilon = 1e-05
SIDE = 4
BLOCKS = 16
GROUP = 4
CHUNK = 16
OFFSETS = (
    (0, 0), (2, 2), (1, 2), (3, 2),
    (2, 1), (2, 3), (1, 1), (3, 3),
    (1, 3), (3, 1), (2, 0), (0, 2),
    (1, 0), (3, 0), (0, 1), (0, 3),
)


def kernel(
    cap, tokens_hbm, meta_ref, gain_ref, gate_hbm, up_hbm, down_hbm, out_ref,
    tokens, normed, cols, slots, send, recv, res, ret, wgu, wd, act, acc,
    load_sem, gu_sem, send_sem, recv_sem, back_sem, ret_sem,
):
    rows, width = tokens.shape
    hidden = wd.shape[0]
    tiles = hidden // 128
    groups = BLOCKS // GROUP
    span = GROUP * cap
    me = lax.axis_index("expert")
    ex, ey = me % SIDE, me // SIDE

    def peer(i, sign):
        dx, dy = OFFSETS[i]
        return ((ey + sign * dy + SIDE) % SIDE) * SIDE + (ex + sign * dx + SIDE) % SIDE

    barrier = pltpu.get_barrier_semaphore()
    for i in range(1, BLOCKS):
        pl.semaphore_signal(barrier, inc=1, device_id={"expert": peer(i, 1)}, device_id_type=MESH)

    load = pltpu.make_async_copy(tokens_hbm, tokens, load_sem.at[0])
    load.start()
    loads = []
    for t in range(tiles):
        for half, source in enumerate((gate_hbm, up_hbm)):
            loads.append(
                pltpu.make_async_copy(
                    source.at[:, pl.ds(t * 128, 128)],
                    wgu.at[:, pl.ds(t * 256 + half * 128, 128)],
                    gu_sem.at[2 * t + half],
                )
            )
    loads.append(pltpu.make_async_copy(down_hbm, wd, load_sem.at[1]))
    for copy in loads:
        copy.start()

    id0, id1 = meta_ref[0:1, :], meta_ref[1:2, :]
    w0, w1 = meta_ref[2:3, :], meta_ref[3:4, :]
    experts = lax.broadcasted_iota(jnp.int32, (BLOCKS, rows), 0).astype(jnp.float32)
    is0, is1 = experts == id0, experts == id1
    names = jnp.where(is0 | is1, 1.0, 0.0).astype(jnp.bfloat16)
    before = lax.broadcasted_iota(jnp.int32, (rows, rows), 0) < lax.broadcasted_iota(jnp.int32, (rows, rows), 1)
    earlier = jnp.dot(names, jnp.where(before, 1.0, 0.0).astype(jnp.bfloat16), preferred_element_type=jnp.float32)
    pos0 = jnp.sum(jnp.where(is0, earlier, 0.0), axis=0, keepdims=True)
    pos1 = jnp.sum(jnp.where(is1, earlier, 0.0), axis=0, keepdims=True)
    base0, base1 = jnp.zeros_like(id0), jnp.zeros_like(id1)
    for i in range(1, BLOCKS):
        name = peer(i, 1).astype(jnp.float32)
        base0 = jnp.where(id0 == name, float(i * cap), base0)
        base1 = jnp.where(id1 == name, float(i * cap), base1)
    slot0, slot1 = base0 + pos0, base1 + pos1
    hi0, hi1 = w0.astype(jnp.bfloat16).astype(jnp.float32), w1.astype(jnp.bfloat16).astype(jnp.float32)
    slots[0:1, :] = slot0.astype(jnp.int32)
    slots[1:2, :] = slot1.astype(jnp.int32)
    table = jnp.concatenate([slot0, slot1, hi0, hi1, w0 - hi0, w1 - hi1, meta_ref[4:5, :], jnp.zeros_like(id0)], axis=0)
    cols[...] = jnp.concatenate([table, jnp.zeros((120, rows), jnp.float32)], axis=0).T

    load.wait()
    step = 64

    def norm_step(r, carry):
        at = pl.ds(pl.multiple_of(r * step, step), step)
        values = tokens[at, :].astype(jnp.float32)
        square = jnp.mean(values * values, axis=1, keepdims=True)
        gains = jnp.where(cols[at, 6:7] == 1.0, gain_ref[1:2, :], gain_ref[0:1, :])
        normed[at, :] = (values * lax.rsqrt(square + epsilon) * gains).astype(jnp.bfloat16)
        return carry

    lax.fori_loop(0, rows // step, norm_step, 0)

    def parts(source, target, sems, rsems, i, device):
        return [
            pltpu.make_async_remote_copy(
                src_ref=source.at[i, pl.ds(c * CHUNK, CHUNK), :],
                dst_ref=target.at[i, pl.ds(c * CHUNK, CHUNK), :],
                send_sem=sems.at[i],
                recv_sem=rsems.at[i],
                device_id={"expert": device},
                device_id_type=MESH,
            )
            for c in range(cap // CHUNK)
        ]

    def whole(source, target, sems, rsems, i, device):
        return pltpu.make_async_remote_copy(
            src_ref=source.at[i],
            dst_ref=target.at[i],
            send_sem=sems.at[i],
            recv_sem=rsems.at[i],
            device_id={"expert": device},
            device_id_type=MESH,
        )

    def start_all(source, target, sems, rsems, blocks, sign):
        lists = [parts(source, target, sems, rsems, i, peer(i, sign)) for i in blocks]
        for c in range(cap // CHUNK):
            for copies in lists:
                copies[c].start()

    for g in range(groups):
        place = lax.broadcasted_iota(jnp.int32, (span, rows), 0) + g * span
        pick = jnp.where((place == slots[0:1, :]) | (place == slots[1:2, :]), 1.0, 0.0).astype(jnp.bfloat16)
        half = width // 4

        def pack_step(n, carry):
            at = pl.ds(pl.multiple_of(n * half, half), half)
            packed = jnp.dot(pick, normed[:, at], preferred_element_type=jnp.float32).astype(jnp.bfloat16)
            packed = packed.reshape(GROUP, cap, half)
            if g == 0:
                recv[0:1, :, at] = packed[0:1]
                send[1:GROUP, :, at] = packed[1:]
            else:
                send[g * GROUP : (g + 1) * GROUP, :, at] = packed
            return carry

        lax.fori_loop(0, 4, pack_step, 0)
        if g == 0:
            pl.semaphore_wait(barrier, BLOCKS - 1)
        start_all(send, recv, send_sem, recv_sem, [i for i in range(g * GROUP, (g + 1) * GROUP) if i], 1)

    for copy in loads:
        copy.wait()

    for g in range(groups):
        blocks = [i for i in range(g * GROUP, (g + 1) * GROUP) if i]
        for i in blocks:
            whole(send, recv, send_sem, recv_sem, i, peer(i, 1)).wait_recv()

        def hidden_step(t, carry):
            at = pl.ds(pl.multiple_of(t * 256, 256), 256)
            flat = recv[g * GROUP : (g + 1) * GROUP].reshape(span, width)
            both = jnp.dot(flat, wgu[:, at], preferred_element_type=jnp.float32)
            gate, upper = both[:, :128], both[:, 128:]
            act[:, pl.ds(pl.multiple_of(t * 128, 128), 128)] = (jax.nn.silu(gate) * upper).astype(jnp.bfloat16)
            return carry

        lax.fori_loop(0, tiles, hidden_step, 0)

        def down_step(n, carry):
            at = pl.ds(pl.multiple_of(n * 256, 256), 256)
            done = jnp.dot(act[...], wd[:, at], preferred_element_type=jnp.float32).astype(jnp.bfloat16)
            done = done.reshape(GROUP, cap, 256)
            if g == 0:
                ret[0:1, :, at] = done[0:1]
                res[1:GROUP, :, at] = done[1:]
            else:
                res[g * GROUP : (g + 1) * GROUP, :, at] = done
            return carry

        lax.fori_loop(0, width // 256, down_step, 0)
        start_all(res, ret, back_sem, ret_sem, blocks, -1)

    for g in range(groups):
        blocks = [i for i in range(g * GROUP, (g + 1) * GROUP) if i]
        for i in blocks:
            whole(res, ret, back_sem, ret_sem, i, peer(i, -1)).wait_recv()
        place = (lax.broadcasted_iota(jnp.int32, (rows, span), 1) + g * span).astype(jnp.float32)
        at0, at1 = place == cols[:, 0:1], place == cols[:, 1:2]
        high = (jnp.where(at0, cols[:, 2:3], 0.0) + jnp.where(at1, cols[:, 3:4], 0.0)).astype(jnp.bfloat16)
        low = (jnp.where(at0, cols[:, 4:5], 0.0) + jnp.where(at1, cols[:, 5:6], 0.0)).astype(jnp.bfloat16)

        def mix_step(n, carry):
            at = pl.ds(pl.multiple_of(n * 256, 256), 256)
            block = ret[g * GROUP : (g + 1) * GROUP, :, at].reshape(span, 256)
            total = jnp.dot(high, block, preferred_element_type=jnp.float32)
            total = total + jnp.dot(low, block, preferred_element_type=jnp.float32)
            if g > 0:
                total = total + acc[:, at]
            if g < groups - 1:
                acc[:, at] = total
            else:
                out_ref[:, at] = (tokens[:, at].astype(jnp.float32) + total).astype(jnp.bfloat16)
            return carry

        lax.fori_loop(0, width // 256, mix_step, 0)

    for i in range(1, BLOCKS):
        whole(send, recv, send_sem, recv_sem, i, peer(i, 1)).wait_send()
        whole(res, ret, back_sem, ret_sem, i, peer(i, -1)).wait_send()


def shards(tokens, modality, expert_ids, route_weights, norm_gain, gate_weight, up_weight, down_weight):
    rows, width = tokens.shape
    fanout = expert_ids.shape[1]
    hidden = down_weight.shape[0]
    cap = min(rows, rows * fanout * 5 // (4 * BLOCKS))
    meta = jnp.concatenate(
        [
            expert_ids.T.astype(jnp.float32),
            route_weights.T,
            modality[None, :].astype(jnp.float32),
            jnp.zeros((3, rows), jnp.float32),
        ],
        axis=0,
    )
    anywhere = pl.BlockSpec(memory_space=pl.ANY)
    vmem = pl.BlockSpec(memory_space=pltpu.VMEM)
    block = pltpu.VMEM((BLOCKS, cap, width), jnp.bfloat16)
    sems = pltpu.SemaphoreType.DMA((BLOCKS,))
    return pl.pallas_call(
        functools.partial(kernel, cap),
        out_shape=jax.ShapeDtypeStruct((rows, width), jnp.bfloat16),
        in_specs=[anywhere, vmem, vmem, anywhere, anywhere, anywhere],
        out_specs=vmem,
        scratch_shapes=[
            pltpu.VMEM((rows, width), jnp.bfloat16),
            pltpu.VMEM((rows, width), jnp.bfloat16),
            pltpu.VMEM((rows, 128), jnp.float32),
            pltpu.VMEM((8, rows), jnp.int32),
            block, block, block, block,
            pltpu.VMEM((width, 2 * hidden), jnp.bfloat16),
            pltpu.VMEM((hidden, width), jnp.bfloat16),
            pltpu.VMEM((GROUP * cap, hidden), jnp.bfloat16),
            pltpu.VMEM((rows, width), jnp.float32),
            pltpu.SemaphoreType.DMA((2,)),
            pltpu.SemaphoreType.DMA((2 * (hidden // 128),)),
            sems, sems, sems, sems,
        ],
        compiler_params=pltpu.CompilerParams(
            collective_id=0, has_side_effects=True, vmem_limit_bytes=62 * 1024 * 1024
        ),
    )(tokens, meta, norm_gain, gate_weight, up_weight, down_weight)


def solution(mesh):
    placed = (
        P(("dp", "expert"), None),
        P(("dp", "expert")),
        P(("dp", "expert"), None),
        P(("dp", "expert"), None),
        P(),
        P(None, "expert"),
        P(None, "expert"),
        P("expert", None),
    )
    return jax.shard_map(
        shards, mesh=mesh, in_specs=placed, out_specs=P(("dp", "expert"), None), check_vma=False
    )
```

time: 244 us -> 149 us (0.61)
  the two profiles are of different devices: /device:TPU:1 before, /device:TPU:10 now
where the time goes in v1:
time: 149 us
  Pallas kernels  143 us (96%)
  local copies, waits for them, and re-layouts  3.24 us (2%)
  other arithmetic  2.73 us (2%)
    pallas_call x1, Pallas kernels, shards(): pl.pallas_call(functools.partial(kernel, cap), out_shape=jax.ShapeDtypeSt...  143 us
    unnamed x1, local copies, waits for them, and re-layouts  3.16 us

profile of v1, /device:TPU:10, one launch (start us, length us, event | category | flops | bytes accessed | tf_op | source)
XLA Modules:
  0.0 148.6 jit_solution(16857065885785403625)
XLA Ops:
  0.0 0.1 pad.3.clone
  0.1 0.7 convert_element_type.14
  0.8 0.7 convert_bitcast_fusion
  1.5 1.4 maximum_maximum_fusion.meta_ref
  2.8 142.6 %shard_map.82 = bf16[512,2048]{1,0:T(8,128)(2,1)} custom-call(bf16[512,2048]{1,0:T(8,128)(2,1)} %tokens_hbm.1, f32[8,512]{1,0:T(8,128)} %maximum_maximum_fusion.meta_ref, f32[2,2048]{1,0:T(2,128)} %gain_ref.1, bf16[2048,896]{1,0:T(8,128)(2,1)} %gate_hbm.1, bf16[2048,896]{1,0:T(8,128)(2,1)} %up_hbm.1, bf16[896,2048]{1,0:T(8,128)(2,1)} %down_hbm.1), custom_call_target="tpu_custom_call" | custom-call | tf_op jit(solution)/shard_map/pallas_call | solution.py:224
  145.4 3.2 %copy.10 = bf16[512,2048]{1,0:T(8,128)(2,1)} copy(bf16[512,2048]{1,0:T(8,128)(2,1)} %shard_map.82) | data formatting | bytes 4194304
  (1 shorter events, 0.0 us)

commit v2 on v1

v2 whole, which is shorter than its diff:
```python
import functools

import jax
import jax.numpy as jnp
from jax import lax
from jax.experimental import pallas as pl
from jax.experimental.pallas import tpu as pltpu
from jax.sharding import PartitionSpec as P

MESH = pl.DeviceIdType.MESH
epsilon = 1e-05
SIDE = 4
BLOCKS = 16
PACK = 4
CHUNK = 16
RING = 8
OFFSETS = (
    (0, 0), (1, 1), (3, 3), (1, 3),
    (3, 1), (2, 0), (0, 2), (1, 0),
    (3, 0), (0, 1), (0, 3), (2, 1),
    (2, 3), (1, 2), (3, 2), (2, 2),
)
OWN = 11
HOSTS = OFFSETS[:OWN] + tuple(((dx + 2) % SIDE, (dy + 2) % SIDE) for dx, dy in OFFSETS[OWN:])
REMOTE = range(1, BLOCKS - 1)
FFN_GROUPS = ((0, 4), (4, 8), (8, 11), (11, 16))
UPWARD = (4, 3, 4)


def kernel(
    cap, ids_ref, weights_ref, modality_ref, gain_ref, tokens_hbm, gate_hbm, up_hbm, down_hbm, out_ref,
    tokens, normed, cols, slots, send, recv, res, ret, own_gate, own_up, own_down,
    far_gate, far_up, far_down, act, acc,
    load_sem, send_sem, recv_sem, back_sem, ret_sem,
    pair_send, pair_recv, ring_send, ring_recv, core_send, core_recv,
):
    rows, width = tokens.shape
    hidden = own_down.shape[0]
    tiles = hidden // 128
    me = lax.axis_index("expert")
    ex, ey = me % SIDE, me // SIDE
    dp = lax.axis_index("dp")
    z, core = dp // 2, dp % 2

    def at_offset(offset, sign):
        dx, dy = offset
        return ((ey + sign * dy + SIDE) % SIDE) * SIDE + (ex + sign * dx + SIDE) % SIDE

    def peer(i, sign):
        return at_offset(HOSTS[i], sign)

    pair = at_offset((2, 2), 1)
    other = z * 2 + 1 - core

    def level(s):
        return (z + s + RING) % RING

    barrier = pltpu.get_barrier_semaphore()
    for i in range(1, OWN):
        pl.semaphore_signal(barrier, inc=1, device_id={"expert": peer(i, 1)}, device_id_type=MESH)
    pl.semaphore_signal(barrier, inc=1, device_id={"expert": pair}, device_id_type=MESH)
    for s in (1, -1):
        pl.semaphore_signal(barrier, inc=1, device_id={"dp": level(s) * 2 + core}, device_id_type=MESH)
    pl.semaphore_signal(barrier, inc=1, device_id={"dp": other}, device_id_type=MESH)

    load = pltpu.make_async_copy(tokens_hbm, tokens, load_sem.at[0])
    load.start()
    loads = [
        pltpu.make_async_copy(gate_hbm, own_gate, load_sem.at[1]),
        pltpu.make_async_copy(up_hbm, own_up, load_sem.at[2]),
        pltpu.make_async_copy(down_hbm, own_down, load_sem.at[3]),
    ]

    def piece(j, k):
        if j == 2:
            return far_down.at[k]
        return (far_gate, far_up)[j].at[pl.ds(pl.multiple_of(k * 128, 128), 128), :]

    def source_piece(j):
        at = pl.ds(pl.multiple_of(dp * 128, 128), 128)
        return (gate_hbm.at[at, :], up_hbm.at[at, :], down_hbm.at[:, at])[j]

    def pair_copy(j):
        return pltpu.make_async_remote_copy(
            src_ref=source_piece(j), dst_ref=piece(j, dp), send_sem=pair_send.at[j], recv_sem=pair_recv.at[j],
            device_id={"expert": pair}, device_id_type=MESH,
        )

    def ring_copy(j, up, s, origin):
        n = (j * 2 + (0 if up else 1)) * 4 + s - 1
        k = origin * 2 + core
        return pltpu.make_async_remote_copy(
            src_ref=piece(j, k), dst_ref=piece(j, k), send_sem=ring_send.at[n], recv_sem=ring_recv.at[n],
            device_id={"dp": level(1 if up else -1) * 2 + core}, device_id_type=MESH,
        )

    def core_copy(j, n, k):
        return pltpu.make_async_remote_copy(
            src_ref=piece(j, k), dst_ref=piece(j, k), send_sem=core_send.at[j * RING + n],
            recv_sem=core_recv.at[j * RING + n], device_id={"dp": other}, device_id_type=MESH,
        )

    def limit(j, up):
        return UPWARD[j] if up else RING - 1 - UPWARD[j]

    def place(up, s):
        return 0 if s == 0 else (s if up else 4 + s)

    core_slots = {}
    for j in range(3):
        found = [(0, 0)] + [(s, -s) for s in range(1, limit(j, True) + 1)]
        found += [(limit(j, True) + s, s) for s in range(1, limit(j, False) + 1)]
        core_slots[j] = found
    sent = []

    def forward(j, up, s):
        if s == 0:
            pair_copy(j).wait_recv()
            n, origin = 0, level(0)
            for way in (True, False):
                copy = ring_copy(j, way, 1, origin)
                copy.start()
                sent.append(copy)
        else:
            origin = level(-s if up else s)
            ring_copy(j, up, s, origin).wait_recv()
            n = s if up else limit(j, True) + s
            if s < limit(j, up):
                copy = ring_copy(j, up, s + 1, origin)
                copy.start()
                sent.append(copy)
        copy = core_copy(j, n, origin * 2 + core)
        copy.start()
        sent.append(copy)

    events = [(j, True, 0) for j in range(3)]
    for s in range(1, 5):
        for j in range(3):
            events += [(j, up, s) for up in (True, False) if s <= limit(j, up)]
    pending = iter(events)

    def advance(count):
        for _ in range(count):
            event = next(pending, None)
            if event is not None:
                forward(*event)

    pl.semaphore_wait(barrier, OWN + 3)
    for j in range(3):
        pair_copy(j).start()
    for copy in loads:
        copy.start()

    id0, id1 = ids_ref[0:1, :], ids_ref[1:2, :]
    w0, w1 = weights_ref[0:1, :], weights_ref[1:2, :]
    experts = lax.broadcasted_iota(jnp.int32, (BLOCKS, rows), 0)
    is0, is1 = experts == id0, experts == id1
    names = jnp.where(is0 | is1, 1.0, 0.0).astype(jnp.bfloat16)
    before = lax.broadcasted_iota(jnp.int32, (rows, rows), 0) < lax.broadcasted_iota(jnp.int32, (rows, rows), 1)
    earlier = jnp.dot(names, jnp.where(before, 1.0, 0.0).astype(jnp.bfloat16), preferred_element_type=jnp.float32)
    pos0 = jnp.sum(jnp.where(is0, earlier, 0.0), axis=0, keepdims=True)
    pos1 = jnp.sum(jnp.where(is1, earlier, 0.0), axis=0, keepdims=True)
    base0, base1 = jnp.zeros_like(pos0), jnp.zeros_like(pos1)
    for i in range(1, BLOCKS):
        name = at_offset(OFFSETS[i], 1)
        base0 = jnp.where(id0 == name, float(i * cap), base0)
        base1 = jnp.where(id1 == name, float(i * cap), base1)
    slot0, slot1 = base0 + pos0, base1 + pos1
    hi0, hi1 = w0.astype(jnp.bfloat16).astype(jnp.float32), w1.astype(jnp.bfloat16).astype(jnp.float32)
    slots[0:1, :] = slot0.astype(jnp.int32)
    slots[1:2, :] = slot1.astype(jnp.int32)
    kind = modality_ref[...].astype(jnp.float32)
    table = jnp.concatenate([slot0, slot1, hi0, hi1, w0 - hi0, w1 - hi1, kind, jnp.zeros_like(kind)], axis=0)
    cols[...] = jnp.concatenate([table, jnp.zeros((120, rows), jnp.float32)], axis=0).T

    load.wait()
    step = 64

    def norm_step(r, carry):
        at = pl.ds(pl.multiple_of(r * step, step), step)
        values = tokens[at, :].astype(jnp.float32)
        square = jnp.mean(values * values, axis=1, keepdims=True)
        gains = jnp.where(cols[at, 6:7] == 1.0, gain_ref[1:2, :], gain_ref[0:1, :])
        normed[at, :] = (values * lax.rsqrt(square + epsilon) * gains).astype(jnp.bfloat16)
        return carry

    lax.fori_loop(0, rows // step, norm_step, 0)

    def parts(source, target, sems, rsems, i, device):
        return [
            pltpu.make_async_remote_copy(
                src_ref=source.at[i, pl.ds(c * CHUNK, CHUNK), :],
                dst_ref=target.at[i, pl.ds(c * CHUNK, CHUNK), :],
                send_sem=sems.at[i],
                recv_sem=rsems.at[i],
                device_id={"expert": device},
                device_id_type=MESH,
            )
            for c in range(cap // CHUNK)
        ]

    def whole(source, target, sems, rsems, i, device):
        return pltpu.make_async_remote_copy(
            src_ref=source.at[i],
            dst_ref=target.at[i],
            send_sem=sems.at[i],
            recv_sem=rsems.at[i],
            device_id={"expert": device},
            device_id_type=MESH,
        )

    def start_all(source, target, sems, rsems, blocks, sign):
        lists = [parts(source, target, sems, rsems, i, peer(i, sign)) for i in blocks]
        for c in range(cap // CHUNK):
            for copies in lists:
                copies[c].start()

    def store(first, last, values, at, remote, local):
        values = values.reshape(last - first, cap, values.shape[-1])
        low, high = max(first, 1), min(last, BLOCKS - 1)
        if first < low:
            local[0:1, :, at] = values[0:1]
        if last > high:
            local[high:last, :, at] = values[high - first :]
        remote[low:high, :, at] = values[low - first : high - first]

    def pack(first, last):
        span = (last - first) * cap
        places = lax.broadcasted_iota(jnp.int32, (span, rows), 0) + first * cap
        pick = jnp.where((places == slots[0:1, :]) | (places == slots[1:2, :]), 1.0, 0.0).astype(jnp.bfloat16)
        part = width // 4

        def pack_step(n, carry):
            at = pl.ds(pl.multiple_of(n * part, part), part)
            packed = jnp.dot(pick, normed[:, at], preferred_element_type=jnp.float32).astype(jnp.bfloat16)
            store(first, last, packed, at, send, recv)
            return carry

        lax.fori_loop(0, 4, pack_step, 0)
        start_all(send, recv, send_sem, recv_sem, [i for i in range(first, last) if i in REMOTE], 1)

    def wait_blocks(first, last, returning):
        for i in range(first, last):
            if i in REMOTE:
                if returning:
                    whole(res, ret, back_sem, ret_sem, i, peer(i, -1)).wait_recv()
                else:
                    whole(send, recv, send_sem, recv_sem, i, peer(i, 1)).wait_recv()

    def ffn_hidden(first, last, gate_w, up_w):
        span = (last - first) * cap

        def hidden_step(t, carry):
            at = pl.ds(pl.multiple_of(t * 128, 128), 128)
            flat = recv[first:last].reshape(span, width)
            weights = jnp.concatenate([gate_w[:, at], up_w[:, at]], axis=1)
            both = jnp.dot(flat, weights, preferred_element_type=jnp.float32)
            gate, upper = both[:, :128], both[:, 128:]
            act[0:span, at] = (jax.nn.silu(gate) * upper).astype(jnp.bfloat16)
            return carry

        lax.fori_loop(0, tiles, hidden_step, 0)

    def ffn_down(first, last, down_w):
        span = (last - first) * cap

        def down_step(n, carry):
            at = pl.ds(pl.multiple_of(n * 256, 256), 256)
            done = jnp.dot(act[0:span, :], down_w(n, at), preferred_element_type=jnp.float32)
            store(first, last, done.astype(jnp.bfloat16), at, res, ret)
            return carry

        lax.fori_loop(0, width // 256, down_step, 0)
        start_all(res, ret, back_sem, ret_sem, [i for i in range(first, last) if i in REMOTE], -1)

    def mix(first, last, begin, end):
        span = (last - first) * cap
        places = (lax.broadcasted_iota(jnp.int32, (rows, span), 1) + first * cap).astype(jnp.float32)
        at0, at1 = places == cols[:, 0:1], places == cols[:, 1:2]
        high = (jnp.where(at0, cols[:, 2:3], 0.0) + jnp.where(at1, cols[:, 3:4], 0.0)).astype(jnp.bfloat16)
        low = (jnp.where(at0, cols[:, 4:5], 0.0) + jnp.where(at1, cols[:, 5:6], 0.0)).astype(jnp.bfloat16)

        def mix_step(n, carry):
            at = pl.ds(pl.multiple_of(n * 256, 256), 256)
            block = ret[first:last, :, at].reshape(span, 256)
            total = jnp.dot(high, block, preferred_element_type=jnp.float32)
            total = total + jnp.dot(low, block, preferred_element_type=jnp.float32)
            if not begin:
                total = total + acc[:, at]
            if end:
                out_ref[:, at] = (tokens[:, at].astype(jnp.float32) + total).astype(jnp.bfloat16)
            else:
                acc[:, at] = total
            return carry

        lax.fori_loop(0, width // 256, mix_step, 0)

    pack(0, 4)
    advance(1)
    pack(4, 8)
    advance(1)
    pack(8, 12)
    advance(1)
    pack(12, 16)

    for copy in loads:
        copy.wait()
    own_columns = lambda n, at: own_down[:, at]
    for first, last in FFN_GROUPS[:3]:
        wait_blocks(first, last, False)
        ffn_hidden(first, last, own_gate, own_up)
        advance(2)
        ffn_down(first, last, own_columns)
        advance(2)
    advance(2)
    wait_blocks(0, 4, True)
    mix(0, 4, True, False)
    advance(len(events))

    for j in range(3):
        for n, origin in core_slots[j]:
            core_copy(j, n, level(origin) * 2 + 1 - core).wait_recv()
    far_columns = lambda n, at: jnp.concatenate([far_down[2 * n], far_down[2 * n + 1]], axis=1)
    wait_blocks(11, 16, False)
    ffn_hidden(11, 16, far_gate, far_up)
    ffn_down(11, 16, far_columns)
    wait_blocks(4, 8, True)
    mix(4, 8, False, False)
    wait_blocks(8, 11, True)
    mix(8, 11, False, False)
    wait_blocks(11, 16, True)
    mix(11, 16, False, True)

    for i in REMOTE:
        whole(send, recv, send_sem, recv_sem, i, peer(i, 1)).wait_send()
        whole(res, ret, back_sem, ret_sem, i, peer(i, -1)).wait_send()
    for j in range(3):
        pair_copy(j).wait_send()
    for copy in sent:
        copy.wait_send()


def shards(tokens, modality, expert_ids, route_weights, norm_gain, gate_weight, up_weight, down_weight):
    rows, width = tokens.shape
    fanout = expert_ids.shape[1]
    hidden = down_weight.shape[0]
    cap = min(rows, rows * fanout * 5 // (4 * BLOCKS))
    anywhere = pl.BlockSpec(memory_space=pl.ANY)
    vmem = pl.BlockSpec(memory_space=pltpu.VMEM)
    block = pltpu.VMEM((BLOCKS, cap, width), jnp.bfloat16)
    sems = pltpu.SemaphoreType.DMA((BLOCKS,))
    dma = pltpu.SemaphoreType.DMA
    longest = max(last - first for first, last in FFN_GROUPS)
    return pl.pallas_call(
        functools.partial(kernel, cap),
        out_shape=jax.ShapeDtypeStruct((rows, width), jnp.bfloat16),
        in_specs=[vmem, vmem, vmem, vmem, anywhere, anywhere, anywhere, anywhere],
        out_specs=vmem,
        scratch_shapes=[
            pltpu.VMEM((rows, width), jnp.bfloat16),
            pltpu.VMEM((rows, width), jnp.bfloat16),
            pltpu.VMEM((rows, 128), jnp.float32),
            pltpu.VMEM((8, rows), jnp.int32),
            block, block, block, block,
            pltpu.VMEM((width, hidden), jnp.bfloat16),
            pltpu.VMEM((width, hidden), jnp.bfloat16),
            pltpu.VMEM((hidden, width), jnp.bfloat16),
            pltpu.VMEM((width, hidden), jnp.bfloat16),
            pltpu.VMEM((width, hidden), jnp.bfloat16),
            pltpu.VMEM((width // 128, hidden, 128), jnp.bfloat16),
            pltpu.VMEM((longest * cap, hidden), jnp.bfloat16),
            pltpu.VMEM((rows, width), jnp.float32),
            dma((4,)),
            sems, sems, sems, sems,
            dma((3,)), dma((3,)), dma((24,)), dma((24,)), dma((24,)), dma((24,)),
        ],
        compiler_params=pltpu.CompilerParams(
            collective_id=0, has_side_effects=True, vmem_limit_bytes=63 * 1024 * 1024
        ),
    )(expert_ids.T, route_weights.T, modality[None, :], norm_gain, tokens, gate_weight, up_weight, down_weight)


def solution(mesh):
    placed = (
        P(("dp", "expert"), None),
        P(("dp", "expert")),
        P(("dp", "expert"), None),
        P(("dp", "expert"), None),
        P(),
        P(None, "expert"),
        P(None, "expert"),
        P("expert", None),
    )
    return jax.shard_map(
        shards, mesh=mesh, in_specs=placed, out_specs=P(("dp", "expert"), None), check_vma=False
    )
```

time: 149 us -> 124 us (0.83)
  the two profiles are of different devices: /device:TPU:10 before, /device:TPU:1 now
where the time goes in v2:
time: 124 us
  Pallas kernels  121 us (98%)
  local copies, waits for them, and re-layouts  3.16 us (3%)
    pallas_call x1, Pallas kernels, shards(): pl.pallas_call(functools.partial(kernel, cap), out_shape=jax.ShapeDtypeSt...  121 us
    unnamed x1, local copies, waits for them, and re-layouts  3.16 us

profile of v2, /device:TPU:1, one launch (start us, length us, event | category | flops | bytes accessed | tf_op | source)
XLA Modules:
  0.0 123.7 jit_solution(895876817250419634)
XLA Ops:
  0.0 120.6 %shard_map.82 = bf16[512,2048]{1,0:T(8,128)(2,1)} custom-call(s32[2,512]{1,0:T(2,128)} %bitcast.3, f32[2,512]{1,0:T(2,128)} %bitcast.4, s32[1,512]{1,0:T(1,128)} %bitcast.5, f32[2,2048]{1,0:T(2,128)} %gain_ref.1, bf16[512,2048]{1,0:T(8,128)(2,1)} %tokens_hbm.1, bf16[2048,896]{1,0:T(8,128)(2,1)} %gate_hbm.1, bf16[2048,896]{1,0:T(8,128)(2,1)} %up_hbm.1, ...), custom_call_target="tpu_custom_call" | custom-call | tf_op jit(solution)/shard_map/pallas_call | solution.py:354
  120.6 3.2 %copy.10 = bf16[512,2048]{1,0:T(8,128)(2,1)} copy(bf16[512,2048]{1,0:T(8,128)(2,1)} %shard_map.82) | data formatting | bytes 4194304

commit v3 on v2

--- a/solution.py
+++ b/solution.py
@@ -12,7 +12,6 @@
 SIDE = 4
 BLOCKS = 16
 PACK = 4
-CHUNK = 16
 RING = 8
 OFFSETS = (
     (0, 0), (1, 1), (3, 3), (1, 3),
@@ -30,7 +29,7 @@
 def kernel(
     cap, ids_ref, weights_ref, modality_ref, gain_ref, tokens_hbm, gate_hbm, up_hbm, down_hbm, out_ref,
     tokens, normed, cols, slots, send, recv, res, ret, own_gate, own_up, own_down,
-    far_gate, far_up, far_down, act, acc,
+    far_gate, far_up, far_down, act, acc, picks, own_mix, far_mix,
     load_sem, send_sem, recv_sem, back_sem, ret_sem,
     pair_send, pair_recv, ring_send, ring_recv, core_send, core_recv,
 ):
@@ -166,11 +165,10 @@
         base0 = jnp.where(id0 == name, float(i * cap), base0)
         base1 = jnp.where(id1 == name, float(i * cap), base1)
     slot0, slot1 = base0 + pos0, base1 + pos1
-    hi0, hi1 = w0.astype(jnp.bfloat16).astype(jnp.float32), w1.astype(jnp.bfloat16).astype(jnp.float32)
     slots[0:1, :] = slot0.astype(jnp.int32)
     slots[1:2, :] = slot1.astype(jnp.int32)
     kind = modality_ref[...].astype(jnp.float32)
-    table = jnp.concatenate([slot0, slot1, hi0, hi1, w0 - hi0, w1 - hi1, kind, jnp.zeros_like(kind)], axis=0)
+    table = jnp.concatenate([slot0, slot1, w0, w1, kind, kind, kind, kind], axis=0)
     cols[...] = jnp.concatenate([table, jnp.zeros((120, rows), jnp.float32)], axis=0).T
 
     load.wait()
@@ -180,24 +178,11 @@
         at = pl.ds(pl.multiple_of(r * step, step), step)
         values = tokens[at, :].astype(jnp.float32)
         square = jnp.mean(values * values, axis=1, keepdims=True)
-        gains = jnp.where(cols[at, 6:7] == 1.0, gain_ref[1:2, :], gain_ref[0:1, :])
+        gains = jnp.where(cols[at, 4:5] == 1.0, gain_ref[1:2, :], gain_ref[0:1, :])
         normed[at, :] = (values * lax.rsqrt(square + epsilon) * gains).astype(jnp.bfloat16)
         return carry
 
     lax.fori_loop(0, rows // step, norm_step, 0)
-
-    def parts(source, target, sems, rsems, i, device):
-        return [
-            pltpu.make_async_remote_copy(
-                src_ref=source.at[i, pl.ds(c * CHUNK, CHUNK), :],
-                dst_ref=target.at[i, pl.ds(c * CHUNK, CHUNK), :],
-                send_sem=sems.at[i],
-                recv_sem=rsems.at[i],
-                device_id={"expert": device},
-                device_id_type=MESH,
-            )
-            for c in range(cap // CHUNK)
-        ]
 
     def whole(source, target, sems, rsems, i, device):
         return pltpu.make_async_remote_copy(
@@ -210,10 +195,8 @@
         )
 
     def start_all(source, target, sems, rsems, blocks, sign):
-        lists = [parts(source, target, sems, rsems, i, peer(i, sign)) for i in blocks]
-        for c in range(cap // CHUNK):
-            for copies in lists:
-                copies[c].start()
+        for i in blocks:
+            whole(source, target, sems, rsems, i, peer(i, sign)).start()
 
     def store(first, last, values, at, remote, local):
         values = values.reshape(last - first, cap, values.shape[-1])
@@ -226,13 +209,19 @@
 
     def pack(first, last):
         span = (last - first) * cap
-        places = lax.broadcasted_iota(jnp.int32, (span, rows), 0) + first * cap
-        pick = jnp.where((places == slots[0:1, :]) | (places == slots[1:2, :]), 1.0, 0.0).astype(jnp.bfloat16)
         part = width // 4
+
+        def pick_step(n, carry):
+            places = lax.broadcasted_iota(jnp.int32, (cap, rows), 0) + (first + n) * cap
+            found = (places == slots[0:1, :]) | (places == slots[1:2, :])
+            picks[pl.ds(pl.multiple_of(n * cap, cap), cap), :] = jnp.where(found, 1.0, 0.0).astype(jnp.bfloat16)
+            return carry
+
+        lax.fori_loop(0, last - first, pick_step, 0)
 
         def pack_step(n, carry):
             at = pl.ds(pl.multiple_of(n * part, part), part)
-            packed = jnp.dot(pick, normed[:, at], preferred_element_type=jnp.float32).astype(jnp.bfloat16)
+            packed = jnp.dot(picks[0:span, :], normed[:, at], preferred_element_type=jnp.float32).astype(jnp.bfloat16)
             store(first, last, packed, at, send, recv)
             return carry
 
@@ -273,27 +262,40 @@
         lax.fori_loop(0, width // 256, down_step, 0)
         start_all(res, ret, back_sem, ret_sem, [i for i in range(first, last) if i in REMOTE], -1)
 
-    def mix(first, last, begin, end):
+    def mix_table(first, last, table):
         span = (last - first) * cap
-        places = (lax.broadcasted_iota(jnp.int32, (rows, span), 1) + first * cap).astype(jnp.float32)
-        at0, at1 = places == cols[:, 0:1], places == cols[:, 1:2]
-        high = (jnp.where(at0, cols[:, 2:3], 0.0) + jnp.where(at1, cols[:, 3:4], 0.0)).astype(jnp.bfloat16)
-        low = (jnp.where(at0, cols[:, 4:5], 0.0) + jnp.where(at1, cols[:, 5:6], 0.0)).astype(jnp.bfloat16)
+
+        def table_step(r, carry):
+            at = pl.ds(pl.multiple_of(r * step, step), step)
+            places = (lax.broadcasted_iota(jnp.int32, (step, span), 1) + first * cap).astype(jnp.float32)
+            first_choice = jnp.where(places == cols[at, 0:1], cols[at, 2:3], 0.0)
+            second_choice = jnp.where(places == cols[at, 1:2], cols[at, 3:4], 0.0)
+            table[at, :] = (first_choice + second_choice).astype(jnp.bfloat16)
+            return carry
+
+        lax.fori_loop(0, rows // step, table_step, 0)
+
+    def mix(first, last, table, end):
+        span = (last - first) * cap
 
         def mix_step(n, carry):
             at = pl.ds(pl.multiple_of(n * 256, 256), 256)
             block = ret[first:last, :, at].reshape(span, 256)
-            total = jnp.dot(high, block, preferred_element_type=jnp.float32)
-            total = total + jnp.dot(low, block, preferred_element_type=jnp.float32)
-            if not begin:
-                total = total + acc[:, at]
+            total = jnp.dot(table[...], block, preferred_element_type=jnp.float32)
             if end:
-                out_ref[:, at] = (tokens[:, at].astype(jnp.float32) + total).astype(jnp.bfloat16)
+                out_ref[:, at] = (acc[:, at] + total).astype(jnp.bfloat16)
             else:
-                acc[:, at] = total
+                acc[:, at] = tokens[:, at].astype(jnp.float32) + total
             return carry
 
         lax.fori_loop(0, width // 256, mix_step, 0)
+
+    def core_wait(j):
+        for n, origin in core_slots[j]:
+            core_copy(j, n, level(origin) * 2 + 1 - core).wait_recv()
+
+    own_columns = lambda n, at: own_down[:, at]
+    far_columns = lambda n, at: jnp.concatenate([far_down[2 * n], far_down[2 * n + 1]], axis=1)
 
     pack(0, 4)
     advance(1)
@@ -302,34 +304,38 @@
     pack(8, 12)
     advance(1)
     pack(12, 16)
-
+    advance(2)
+    mix_table(0, OWN, own_mix)
+    mix_table(OWN, BLOCKS, far_mix)
     for copy in loads:
         copy.wait()
-    own_columns = lambda n, at: own_down[:, at]
-    for first, last in FFN_GROUPS[:3]:
-        wait_blocks(first, last, False)
-        ffn_hidden(first, last, own_gate, own_up)
-        advance(2)
-        ffn_down(first, last, own_columns)
-        advance(2)
-    advance(2)
-    wait_blocks(0, 4, True)
-    mix(0, 4, True, False)
-    advance(len(events))
-
-    for j in range(3):
-        for n, origin in core_slots[j]:
-            core_copy(j, n, level(origin) * 2 + 1 - core).wait_recv()
-    far_columns = lambda n, at: jnp.concatenate([far_down[2 * n], far_down[2 * n + 1]], axis=1)
-    wait_blocks(11, 16, False)
-    ffn_hidden(11, 16, far_gate, far_up)
-    ffn_down(11, 16, far_columns)
-    wait_blocks(4, 8, True)
-    mix(4, 8, False, False)
-    wait_blocks(8, 11, True)
-    mix(8, 11, False, False)
-    wait_blocks(11, 16, True)
-    mix(11, 16, False, True)
+    advance(2)
+    wait_blocks(0, 4, False)
+    ffn_hidden(0, 4, own_gate, own_up)
+    advance(2)
+    ffn_down(0, 4, own_columns)
+    advance(4)
+    wait_blocks(4, 8, False)
+    ffn_hidden(4, 8, own_gate, own_up)
+    advance(2)
+    ffn_down(4, 8, own_columns)
+    advance(4)
+    wait_blocks(8, OWN, False)
+    ffn_hidden(8, OWN, own_gate, own_up)
+    advance(2)
+    ffn_down(8, OWN, own_columns)
+    advance(2)
+    core_wait(0)
+    core_wait(1)
+    wait_blocks(OWN, BLOCKS, False)
+    ffn_hidden(OWN, BLOCKS, far_gate, far_up)
+    advance(1)
+    core_wait(2)
+    ffn_down(OWN, BLOCKS, far_columns)
+    wait_blocks(0, OWN, True)
+    mix(0, OWN, own_mix, False)
+    wait_blocks(OWN, BLOCKS, True)
+    mix(OWN, BLOCKS, far_mix, True)
 
     for i in REMOTE:
         whole(send, recv, send_sem, recv_sem, i, peer(i, 1)).wait_send()
@@ -370,6 +376,9 @@
             pltpu.VMEM((width // 128, hidden, 128), jnp.bfloat16),
             pltpu.VMEM((longest * cap, hidden), jnp.bfloat16),
             pltpu.VMEM((rows, width), jnp.float32),
+            pltpu.VMEM((PACK * cap, rows), jnp.bfloat16),
+            pltpu.VMEM((rows, OWN * cap), jnp.bfloat16),
+            pltpu.VMEM((rows, (BLOCKS - OWN) * cap), jnp.bfloat16),
             dma((4,)),
             sems, sems, sems, sems,
             dma((3,)), dma((3,)), dma((24,)), dma((24,)), dma((24,)), dma((24,)),

time: 124 us -> 109 us (0.88)
  Pallas kernels: 121 us -> 105 us
    pallas_call x1, Pallas kernels: 121 us -> 105 us  [shards(): pl.pallas_call(functools.partial(kernel, cap), out_shape=jax.ShapeDtypeSt...]
where the time goes in v3:
time: 109 us; the launch traced here: 108 us
  Pallas kernels  105 us (96%)
  local copies, waits for them, and re-layouts  3.16 us (3%)
    pallas_call x1, Pallas kernels, shards(): pl.pallas_call(functools.partial(kernel, cap), out_shape=jax.ShapeDtypeSt...  105 us
    unnamed x1, local copies, waits for them, and re-layouts  3.16 us

profile of v3, /device:TPU:1, one launch (start us, length us, event | category | flops | bytes accessed | tf_op | source)
XLA Modules:
  0.0 108.4 jit_solution(16403580458746649640)
XLA Ops:
  0.0 105.2 %shard_map.82 = bf16[512,2048]{1,0:T(8,128)(2,1)} custom-call(s32[2,512]{1,0:T(2,128)} %bitcast.3, f32[2,512]{1,0:T(2,128)} %bitcast.4, s32[1,512]{1,0:T(1,128)} %bitcast.5, f32[2,2048]{1,0:T(2,128)} %gain_ref.1, bf16[512,2048]{1,0:T(8,128)(2,1)} %tokens_hbm.1, bf16[2048,896]{1,0:T(8,128)(2,1)} %gate_hbm.1, bf16[2048,896]{1,0:T(8,128)(2,1)} %up_hbm.1, ...), custom_call_target="tpu_custom_call" | custom-call | tf_op jit(solution)/shard_map/pallas_call | solution.py:360
  105.2 3.2 %copy.10 = bf16[512,2048]{1,0:T(8,128)(2,1)} copy(bf16[512,2048]{1,0:T(8,128)(2,1)} %shard_map.82) | data formatting | bytes 4194304

commit v4 on v3

--- a/solution.py
+++ b/solution.py
@@ -27,10 +27,10 @@
 
 
 def kernel(
-    cap, ids_ref, weights_ref, modality_ref, gain_ref, tokens_hbm, gate_hbm, up_hbm, down_hbm, out_ref,
+    cap, ids_ref, weights_ref, modality_ref, gain_ref, tokens_hbm, gate_hbm, up_hbm, down_hbm, out_hbm,
     tokens, normed, cols, slots, send, recv, res, ret, own_gate, own_up, own_down,
     far_gate, far_up, far_down, act, acc, picks, own_mix, far_mix,
-    load_sem, send_sem, recv_sem, back_sem, ret_sem,
+    mixed, load_sem, out_sem, send_sem, recv_sem, back_sem, ret_sem,
     pair_send, pair_recv, ring_send, ring_recv, core_send, core_recv,
 ):
     rows, width = tokens.shape
@@ -283,7 +283,8 @@
             block = ret[first:last, :, at].reshape(span, 256)
             total = jnp.dot(table[...], block, preferred_element_type=jnp.float32)
             if end:
-                out_ref[:, at] = (acc[:, at] + total).astype(jnp.bfloat16)
+                mixed[:, at] = (acc[:, at] + total).astype(jnp.bfloat16)
+                pltpu.make_async_copy(mixed.at[:, at], out_hbm.at[:, at], out_sem.at[n]).start()
             else:
                 acc[:, at] = tokens[:, at].astype(jnp.float32) + total
             return carry
@@ -344,6 +345,22 @@
         pair_copy(j).wait_send()
     for copy in sent:
         copy.wait_send()
+    for n in range(width // 256):
+        at = pl.ds(n * 256, 256)
+        pltpu.make_async_copy(mixed.at[:, at], out_hbm.at[:, at], out_sem.at[n]).wait()
+
+
+def hand_over(source, target, held, in_sem, out_sem):
+    count = held.shape[0]
+    reads = [pltpu.make_async_copy(source.at[n], held.at[n], in_sem.at[n]) for n in range(count)]
+    writes = [pltpu.make_async_copy(held.at[n], target.at[n], out_sem.at[n]) for n in range(count)]
+    for read in reads:
+        read.start()
+    for read, write in zip(reads, writes):
+        read.wait()
+        write.start()
+    for write in writes:
+        write.wait()
 
 
 def shards(tokens, modality, expert_ids, route_weights, norm_gain, gate_weight, up_weight, down_weight):
@@ -357,11 +374,11 @@
     sems = pltpu.SemaphoreType.DMA((BLOCKS,))
     dma = pltpu.SemaphoreType.DMA
     longest = max(last - first for first, last in FFN_GROUPS)
-    return pl.pallas_call(
+    result = pl.pallas_call(
         functools.partial(kernel, cap),
         out_shape=jax.ShapeDtypeStruct((rows, width), jnp.bfloat16),
         in_specs=[vmem, vmem, vmem, vmem, anywhere, anywhere, anywhere, anywhere],
-        out_specs=vmem,
+        out_specs=anywhere,
         scratch_shapes=[
             pltpu.VMEM((rows, width), jnp.bfloat16),
             pltpu.VMEM((rows, width), jnp.bfloat16),
@@ -379,7 +396,9 @@
             pltpu.VMEM((PACK * cap, rows), jnp.bfloat16),
             pltpu.VMEM((rows, OWN * cap), jnp.bfloat16),
             pltpu.VMEM((rows, (BLOCKS - OWN) * cap), jnp.bfloat16),
+            pltpu.VMEM((rows, width), jnp.bfloat16),
             dma((4,)),
+            dma((width // 256,)),
             sems, sems, sems, sems,
             dma((3,)), dma((3,)), dma((24,)), dma((24,)), dma((24,)), dma((24,)),
         ],
@@ -387,6 +406,15 @@
             collective_id=0, has_side_effects=True, vmem_limit_bytes=63 * 1024 * 1024
         ),
     )(expert_ids.T, route_weights.T, modality[None, :], norm_gain, tokens, gate_weight, up_weight, down_weight)
+    pieces = 8
+    shape = (pieces, rows // pieces, width)
+    return pl.pallas_call(
+        hand_over,
+        out_shape=jax.ShapeDtypeStruct(shape, jnp.bfloat16),
+        in_specs=[anywhere],
+        out_specs=anywhere,
+        scratch_shapes=[pltpu.VMEM(shape, jnp.bfloat16), dma((pieces,)), dma((pieces,))],
+    )(result.reshape(shape)).reshape(rows, width)
 
 
 def solution(mesh):

time: 109 us -> 107 us (0.982)
  local copies, waits for them, and re-layouts: 3.16 us -> 0 us
  Pallas kernels: 105 us -> 107 us
    unnamed x1 -> x0, local copies, waits for them, and re-layouts: 3.16 us -> none
    pallas_call x0 -> x1, Pallas kernels: none -> 2.39 us  [shards(): pl.pallas_call(hand_over, out_shape=jax.ShapeDtypeStruct(shape, jnp.bfloa...]
where the time goes in v4:
time: 107 us
  Pallas kernels  107 us (100%)
    pallas_call x1, Pallas kernels, shards(): pl.pallas_call(functools.partial(kernel, cap), out_shape=jax.ShapeDtypeSt...  105 us
    pallas_call x1, Pallas kernels, shards(): pl.pallas_call(hand_over, out_shape=jax.ShapeDtypeStruct(shape, jnp.bfloa...  2.39 us

profile of v4, /device:TPU:1, one launch (start us, length us, event | category | flops | bytes accessed | tf_op | source)
XLA Modules:
  0.0 107.0 jit_solution(11973364756915824925)
XLA Ops:
  0.0 104.6 %shard_map.82 = bf16[512,2048]{1,0:T(8,128)(2,1)} custom-call(s32[2,512]{1,0:T(2,128)} %bitcast.6, f32[2,512]{1,0:T(2,128)} %bitcast.7, s32[1,512]{1,0:T(1,128)} %bitcast.8, f32[2,2048]{1,0:T(2,128)} %gain_ref.1, bf16[512,2048]{1,0:T(8,128)(2,1)} %tokens_hbm.1, bf16[2048,896]{1,0:T(8,128)(2,1)} %gate_hbm.1, bf16[2048,896]{1,0:T(8,128)(2,1)} %up_hbm.1, ...), custom_call_target="tpu_custom_call" | custom-call | tf_op jit(solution)/shard_map/pallas_call | solution.py:377
  104.6 2.4 %shard_map.83 = bf16[8,64,2048]{2,1,0:T(8,128)(2,1)} custom-call(bf16[8,64,2048]{2,1,0:T(8,128)(2,1)} %bitcast.5), custom_call_target="tpu_custom_call" | custom-call | tf_op jit(solution)/shard_map/pallas_call | solution.py:411

commit v5 on v4

--- a/solution.py
+++ b/solution.py
@@ -31,7 +31,7 @@
     tokens, normed, cols, slots, send, recv, res, ret, own_gate, own_up, own_down,
     far_gate, far_up, far_down, act, acc, picks, own_mix, far_mix,
     mixed, load_sem, out_sem, send_sem, recv_sem, back_sem, ret_sem,
-    pair_send, pair_recv, ring_send, ring_recv, core_send, core_recv,
+    pair_send, pair_recv, ring_send, ring_recv, core_send, core_recv, chain,
 ):
     rows, width = tokens.shape
     hidden = own_down.shape[0]
@@ -58,9 +58,17 @@
     for i in range(1, OWN):
         pl.semaphore_signal(barrier, inc=1, device_id={"expert": peer(i, 1)}, device_id_type=MESH)
     pl.semaphore_signal(barrier, inc=1, device_id={"expert": pair}, device_id_type=MESH)
-    for s in (1, -1):
-        pl.semaphore_signal(barrier, inc=1, device_id={"dp": level(s) * 2 + core}, device_id_type=MESH)
     pl.semaphore_signal(barrier, inc=1, device_id={"dp": other}, device_id_type=MESH)
+
+    @pl.when(z < RING - 1)
+    def _():
+        pl.semaphore_signal(barrier, inc=1, device_id={"dp": level(1) * 2 + core}, device_id_type=MESH)
+
+    @pl.when(z > 0)
+    def _():
+        pl.semaphore_signal(barrier, inc=1, device_id={"dp": level(-1) * 2 + core}, device_id_type=MESH)
+
+    neighbours = (z + RING - 1) // RING + (2 * (RING - 1) - z) // RING
 
     load = pltpu.make_async_copy(tokens_hbm, tokens, load_sem.at[0])
     load.start()
@@ -116,10 +124,16 @@
         if s == 0:
             pair_copy(j).wait_recv()
             n, origin = 0, level(0)
-            for way in (True, False):
-                copy = ring_copy(j, way, 1, origin)
-                copy.start()
-                sent.append(copy)
+            copy = ring_copy(j, True, 1, origin)
+            copy.start()
+            sent.append(copy)
+            down = ring_copy(j, False, 1, origin)
+            sent.append(down)
+
+            @pl.when(z > 0)
+            def _():
+                down.start()
+
         else:
             origin = level(-s if up else s)
             ring_copy(j, up, s, origin).wait_recv()
@@ -143,12 +157,26 @@
             event = next(pending, None)
             if event is not None:
                 forward(*event)
-
-    pl.semaphore_wait(barrier, OWN + 3)
+            if event == (0, True, 1):
+
+                @pl.when(z == 0)
+                def _():
+                    for j in range(3):
+                        ring_copy(j, False, 1, level(0)).start()
+
+    pl.semaphore_wait(barrier, OWN + 1 + neighbours)
     for j in range(3):
         pair_copy(j).start()
     for copy in loads:
         copy.start()
+
+    @pl.when(z > 0)
+    def _():
+        pl.semaphore_wait(chain, 1)
+
+    @pl.when(z < RING - 1)
+    def _():
+        pl.semaphore_signal(chain, inc=1, device_id={"dp": level(1) * 2 + core}, device_id_type=MESH)
 
     id0, id1 = ids_ref[0:1, :], ids_ref[1:2, :]
     w0, w1 = weights_ref[0:1, :], weights_ref[1:2, :]
@@ -401,6 +429,7 @@
             dma((width // 256,)),
             sems, sems, sems, sems,
             dma((3,)), dma((3,)), dma((24,)), dma((24,)), dma((24,)), dma((24,)),
+            pltpu.SemaphoreType.REGULAR,
         ],
         compiler_params=pltpu.CompilerParams(
             collective_id=0, has_side_effects=True, vmem_limit_bytes=63 * 1024 * 1024

time: 107 us -> 107 us (level)
  the two profiles are of different devices: /device:TPU:1 before, /device:TPU:4 now
where the time goes in v5:
time: 107 us
  Pallas kernels  107 us (100%)
    pallas_call x1, Pallas kernels, shards(): pl.pallas_call(functools.partial(kernel, cap), out_shape=jax.ShapeDtypeSt...  105 us
    pallas_call x1, Pallas kernels, shards(): pl.pallas_call(hand_over, out_shape=jax.ShapeDtypeStruct(shape, jnp.bfloa...  2.39 us

profile of v5, /device:TPU:4, one launch (start us, length us, event | category | flops | bytes accessed | tf_op | source)
XLA Modules:
  0.0 106.9 jit_solution(15153314677246699767)
XLA Ops:
  0.0 104.5 %shard_map.82 = bf16[512,2048]{1,0:T(8,128)(2,1)} custom-call(s32[2,512]{1,0:T(2,128)} %bitcast.6, f32[2,512]{1,0:T(2,128)} %bitcast.7, s32[1,512]{1,0:T(1,128)} %bitcast.8, f32[2,2048]{1,0:T(2,128)} %gain_ref.1, bf16[512,2048]{1,0:T(8,128)(2,1)} %tokens_hbm.1, bf16[2048,896]{1,0:T(8,128)(2,1)} %gate_hbm.1, bf16[2048,896]{1,0:T(8,128)(2,1)} %up_hbm.1, ...), custom_call_target="tpu_custom_call" | custom-call | tf_op jit(solution)/shard_map/pallas_call | solution.py:405
  104.5 2.4 %shard_map.83 = bf16[8,64,2048]{2,1,0:T(8,128)(2,1)} custom-call(bf16[8,64,2048]{2,1,0:T(8,128)(2,1)} %bitcast.5), custom_call_target="tpu_custom_call" | custom-call | tf_op jit(solution)/shard_map/pallas_call | solution.py:440

commit v6 on v4

--- a/solution.py
+++ b/solution.py
@@ -312,15 +312,17 @@
         copy.wait()
     advance(2)
     wait_blocks(0, 4, False)
+    advance(1)
     ffn_hidden(0, 4, own_gate, own_up)
     advance(2)
     ffn_down(0, 4, own_columns)
     advance(4)
     wait_blocks(4, 8, False)
+    advance(1)
     ffn_hidden(4, 8, own_gate, own_up)
     advance(2)
     ffn_down(4, 8, own_columns)
-    advance(4)
+    advance(3)
     wait_blocks(8, OWN, False)
     ffn_hidden(8, OWN, own_gate, own_up)
     advance(2)

time: 107 us -> 107 us (level)
  no operation moved by 1% of the time
where the time goes in v6:
time: 107 us
  Pallas kernels  107 us (100%)
    pallas_call x1, Pallas kernels, shards(): pl.pallas_call(functools.partial(kernel, cap), out_shape=jax.ShapeDtypeSt...  105 us
    pallas_call x1, Pallas kernels, shards(): pl.pallas_call(hand_over, out_shape=jax.ShapeDtypeStruct(shape, jnp.bfloa...  2.39 us

profile of v6, /device:TPU:1, one launch (start us, length us, event | category | flops | bytes accessed | tf_op | source)
XLA Modules:
  0.0 107.0 jit_solution(3251927261649808091)
XLA Ops:
  0.0 104.6 %shard_map.82 = bf16[512,2048]{1,0:T(8,128)(2,1)} custom-call(s32[2,512]{1,0:T(2,128)} %bitcast.6, f32[2,512]{1,0:T(2,128)} %bitcast.7, s32[1,512]{1,0:T(1,128)} %bitcast.8, f32[2,2048]{1,0:T(2,128)} %gain_ref.1, bf16[512,2048]{1,0:T(8,128)(2,1)} %tokens_hbm.1, bf16[2048,896]{1,0:T(8,128)(2,1)} %gate_hbm.1, bf16[2048,896]{1,0:T(8,128)(2,1)} %up_hbm.1, ...), custom_call_target="tpu_custom_call" | custom-call | tf_op jit(solution)/shard_map/pallas_call | solution.py:379
  104.6 2.4 %shard_map.83 = bf16[8,64,2048]{2,1,0:T(8,128)(2,1)} custom-call(bf16[8,64,2048]{2,1,0:T(8,128)(2,1)} %bitcast.5), custom_call_target="tpu_custom_call" | custom-call | tf_op jit(solution)/shard_map/pallas_call | solution.py:413
